TPU v7x, 8 devices: a whole 2x2x1 slice. The times are simulated.
8 devices in a mesh: sys: 1 (over z), zdom: 2 (over y), ydom: 4 (over x, core).
Axes of the slice: x: 2, y: 2, z: 1, core: 2. Of those that a mesh axis runs over, the one named last changes fastest.
Arguments:
- charge: float32 [65536], P(('sys', 'ydom', 'zdom'))
- real_mask: int32 [65536], P(('sys', 'ydom', 'zdom'))
- grid_idx: int32 [65536, 3], P(('sys', 'ydom', 'zdom'))
- spline_w: float32 [65536, 3, 4], P(('sys', 'ydom', 'zdom'))
- influence: float32 [128, 128, 128], P(('sys', 'ydom'), 'zdom')
Outputs:
- output 1: float32 [128, 128, 128], P(('sys', 'ydom'), 'zdom')
- output 2: float32 [1], P('sys')
All inputs are finite; a program needn't handle non-finite values.
Results may differ from a plain program's by a relative error of at most 0.001.
Values are sent between devices in bfloat16 or wider.
A program may use at most 1 GiB of HBM per device.

v0:
```python
import functools
import math
import numpy as np
import jax
import jax.numpy as jnp
from jax import lax
from jax.experimental import pallas as pl
from jax.experimental.pallas import tpu as pltpu
from jax.sharding import PartitionSpec as P

MESH = pl.DeviceIdType.MESH
F32 = jnp.float32
BF16 = jnp.bfloat16
GRID = 128
LEN_Y = 32
LEN_Z = 64
GHOST = 3
BLOCK = 256
Y_ROWS = 40
GROUPS = 4
CHUNKS = 4
NT = (((1,), (1,)), ((), ()))
NN = (((1,), (0,)), ((), ()))


def split_table(table):
    table = np.asarray(table, np.float32)
    high = table.astype(jnp.bfloat16)
    low = (table - high.astype(np.float32)).astype(jnp.bfloat16)
    return np.stack([high, low])


def dft_tables():
    k = np.arange(GRID)
    phase = 2.0 * np.pi * ((k[:, None] * k[None, :]) % GRID) / GRID
    cos, sin = np.cos(phase), np.sin(phase)
    x_table = np.concatenate([cos, -sin], axis=0)
    z_table = []
    for half in range(2):
        c = cos[64 * half:64 * half + 64]
        s = sin[64 * half:64 * half + 64]
        z_table.append(np.block([[c, -s], [s, c]]))
    return split_table(x_table), split_table(np.stack(z_table))


def split(value):
    high = value.astype(BF16)
    low = (value - high.astype(F32)).astype(BF16)
    return high, low


def dot(a, b, dims):
    return lax.dot_general(a, b, dims, preferred_element_type=F32)


def taps(base, weights, rows):
    delta = lax.broadcasted_iota(jnp.int32, (rows, base.shape[1]), 0) - base
    out = jnp.where(delta == 3, weights[3:4], 0.0)
    for s in (2, 1, 0):
        out = jnp.where(delta == s, weights[s:s + 1], out)
    return out


def c_add(a, b):
    return a[0] + b[0], a[1] + b[1]


def c_sub(a, b):
    return a[0] - b[0], a[1] - b[1]


def c_mul(a, turn):
    turn = turn % 1.0
    if turn == 0.0:
        return a
    if turn == 0.25:
        return a[1], -a[0]
    if turn == 0.5:
        return -a[0], -a[1]
    if turn == 0.75:
        return -a[1], a[0]
    c, s = math.cos(2 * math.pi * turn), math.sin(2 * math.pi * turn)
    if turn == 0.125:
        return c * (a[0] + a[1]), c * (a[1] - a[0])
    return c * a[0] + s * a[1], c * a[1] - s * a[0]


def fft(values):
    n = len(values)
    if n == 1:
        return values
    even, odd = fft(values[0::2]), fft(values[1::2])
    turned = [c_mul(o, k / n) for k, o in enumerate(odd)]
    return [c_add(e, t) for e, t in zip(even, turned)] + [c_sub(e, t) for e, t in zip(even, turned)]


def kernel(blocks, charge, mask, index, spline, influence, x_table, z_table,
           energy_out, total_out,
           xcat, yline, zline, acc, yghost, zghost, yface, zface, corner,
           fsend, grecv, mid, hbuf, hrecv, evec, erecv,
           ghost_send, ghost_recv, a_send, a_recv, b_send, b_recv, e_send, e_recv):
    i = lax.axis_index('ydom')
    j = lax.axis_index('zdom')
    me = j * 4 + i
    i_next = lax.rem(i + 1, 4)
    j_next = 1 - j

    barrier = pltpu.get_barrier_semaphore()
    for off in range(1, 8):
        peer = lax.rem(me + off, 8)
        pl.semaphore_signal(barrier, inc=1, device_id=(0, peer // 4, lax.rem(peer, 4)), device_id_type=MESH)

    acc[...] = jnp.zeros_like(acc)
    yghost[...] = jnp.zeros_like(yghost)
    zghost[...] = jnp.zeros_like(zghost)

    def prepare(b, carry):
        lanes = pl.ds(pl.multiple_of(b * BLOCK, BLOCK), BLOCK)
        weight = charge[:, lanes] * mask[:, lanes].astype(F32)
        wx = spline[0, :, lanes] * weight
        base = index[0:1, lanes]
        delta = (lax.broadcasted_iota(jnp.int32, (GRID, BLOCK), 0) - base) & (GRID - 1)
        line = jnp.where(delta == 3, wx[3:4], 0.0)
        for s in (2, 1, 0):
            line = jnp.where(delta == s, wx[s:s + 1], line)
        high, low = split(line)
        xcat[b, 0:GRID] = high
        xcat[b, GRID:2 * GRID] = low
        yl = taps(index[1:2, lanes], spline[1, :, lanes], Y_ROWS)
        yline[b] = yl
        zl = taps(index[2:3, lanes], spline[2, :, lanes], LEN_Z + 8)
        zline[b] = zl[0:LEN_Z]
        rows = [yl[LEN_Y + t:LEN_Y + t + 1] * zl[0:LEN_Z] for t in range(GHOST)]
        rows += [zl[LEN_Z + u:LEN_Z + u + 1] * yl for u in range(GHOST)]
        rows += [jnp.zeros((8, BLOCK), F32)]
        high, low = split(jnp.concatenate(rows, axis=0))
        part = dot(high, xcat[b], NT)
        part = part[:, 0:GRID] + part[:, GRID:] + dot(low, xcat[b, 0:GRID], NT)
        yghost[...] += part[0:GHOST * LEN_Z].reshape(GHOST, LEN_Z, GRID)
        zghost[...] += part[GHOST * LEN_Z:GHOST * LEN_Z + GHOST * Y_ROWS].reshape(GHOST, Y_ROWS, GRID)
        return carry

    lax.fori_loop(0, blocks, prepare, 0)

    pl.semaphore_wait(barrier, 7)
    ghosts = []
    for n, (src, dst, peer) in enumerate([
            (yghost, yface, (0, j, i_next)),
            (zghost.at[:, 0:LEN_Y], zface, (0, j_next, i)),
            (zghost.at[:, LEN_Y:Y_ROWS], corner, (0, j_next, i_next))]):
        copy = pltpu.make_async_remote_copy(
            src_ref=src, dst_ref=dst, send_sem=ghost_send.at[n], recv_sem=ghost_recv.at[n],
            device_id=peer, device_id_type=MESH)
        copy.start()
        ghosts.append(copy)

    def spread_rows(group):
        def body(b, carry):
            zl = zline[b]
            yl = yline[b, 8 * group:8 * group + 8]
            xb = xcat[b]
            high, low = split(jnp.concatenate([yl[t:t + 1] * zl for t in range(8)], axis=0))
            part = dot(high, xb, NT)
            acc[...] += part[:, 0:GRID] + part[:, GRID:] + dot(low, xb[0:GRID], NT)
            return carry
        lax.fori_loop(0, blocks, body, 0)

    a_copies = {}
    order = list(range(GROUPS - 1, -1, -1))
    for turn, group in enumerate(order):
        if turn > 0:
            acc[...] = jnp.zeros_like(acc)
        spread_rows(group)
        if turn == 0:
            for copy in ghosts:
                copy.wait_recv()
        if group == 0:
            for t in range(GHOST):
                face = jnp.concatenate(
                    [yface[t, 0:8] + jnp.concatenate(
                        [corner[u, t:t + 1] for u in range(GHOST)] + [jnp.zeros((8 - GHOST, GRID), F32)], axis=0),
                     yface[t, 8:LEN_Z]], axis=0)
                acc[LEN_Z * t:LEN_Z * t + LEN_Z] += face
        for u in range(GHOST):
            acc[pl.ds(u, 8, stride=LEN_Z)] += zface[u, 8 * group:8 * group + 8]
        for pair in range(4):
            high, low = split(acc[128 * pair:128 * pair + 128])
            modes = dot(x_table[0], high, NT) + dot(x_table[1], high, NT) + dot(x_table[0], low, NT)
            fsend[group, 0, pair] = modes[0:GRID]
            fsend[group, 1, pair] = modes[GRID:]
        for chunk in range(CHUNKS):
            for d in (2, 1, 3):
                peer = lax.rem(i + d, 4)
                copy = pltpu.make_async_remote_copy(
                    src_ref=fsend.at[group, :, :, pl.ds(pl.multiple_of(32 * peer + 8 * chunk, 8), 8), :],
                    dst_ref=grecv.at[i, group, chunk],
                    send_sem=a_send.at[group, chunk, d], recv_sem=a_recv.at[group, chunk, d],
                    device_id=(0, j, peer), device_id_type=MESH)
                copy.start()
                a_copies[group, chunk, d] = copy
            grecv[i, group, chunk] = fsend[group, :, :, pl.ds(pl.multiple_of(32 * i + 8 * chunk, 8), 8), :]

    low_half = lax.broadcasted_iota(jnp.int32, (8, GRID), 1) < 64
    b_copies = []
    for chunk in range(CHUNKS):
        for group in range(GROUPS):
            for d in (1, 2, 3):
                a_copies[group, chunk, d].wait_recv()
        for b in range(8):
            values = []
            for a in range(8):
                q = 8 * a + b
                src, group, pair = q // 16, (q % 16) // 4, q % 4
                values.append((grecv[src, group, chunk, 0, pair], grecv[src, group, chunk, 1, pair]))
            for c, value in enumerate(fft(values)):
                value = c_mul(value, b * c / 64)
                mid[c, b, 0] = value[0]
                mid[c, b, 1] = value[1]
        for c in range(8):
            values = fft([(mid[c, b, 0], mid[c, b, 1]) for b in range(8)])
            for d, value in enumerate(values):
                k = c + 8 * d
                turned = c_mul(value, k / 128)
                left = jnp.where(low_half, value[0], pltpu.roll(value[1], 64, 1))
                right = jnp.where(low_half, pltpu.roll(turned[0], 64, 1), turned[1])
                hbuf[chunk, 0, k] = left + right
                hbuf[chunk, 1, k] = left - right
        copy = pltpu.make_async_remote_copy(
            src_ref=hbuf.at[chunk, j_next], dst_ref=hrecv.at[chunk],
            send_sem=b_send.at[chunk], recv_sem=b_recv.at[chunk],
            device_id=(0, j_next, i), device_id_type=MESH)
        copy.start()
        b_copies.append(copy)

    table = [jnp.concatenate([z_table[n, j], z_table[n, j_next]], axis=0) for n in range(2)]
    total = jnp.zeros((8, GRID), F32)
    for chunk in range(CHUNKS):
        b_copies[chunk].wait_recv()
        rows = jnp.concatenate([hbuf[chunk, j].reshape(512, GRID), hrecv[chunk].reshape(512, GRID)], axis=1)
        high, low = split(rows)
        modes = dot(high, table[0], NN) + dot(high, table[1], NN) + dot(low, table[0], NN)
        re, im = modes[:, 0:GRID], modes[:, GRID:]
        power = jnp.transpose((re * re + im * im).reshape(64, 8, GRID), (1, 0, 2))
        mode = 0.5 * influence[8 * chunk:8 * chunk + 8] * power
        energy_out[8 * chunk:8 * chunk + 8] = mode
        total = total + jnp.sum(mode.reshape(64, 8, GRID), axis=0)

    evec[...] = total
    e_copies = []
    for off in range(1, 8):
        peer = lax.rem(me + off, 8)
        copy = pltpu.make_async_remote_copy(
            src_ref=evec, dst_ref=erecv.at[me], send_sem=e_send.at[off], recv_sem=e_recv.at[off],
            device_id=(0, peer // 4, lax.rem(peer, 4)), device_id_type=MESH)
        copy.start()
        e_copies.append(copy)
    erecv[me] = total
    for copy in e_copies:
        copy.wait_recv()
    grand = erecv[0]
    for n in range(1, 8):
        grand = grand + erecv[n]
    total_out[0] = jnp.sum(grand) * (1.0 / (GRID * GRID * GRID))

    for copy in ghosts + list(a_copies.values()) + b_copies + e_copies:
        copy.wait_send()


def solution(mesh):
    slot_spec = P(('sys', 'ydom', 'zdom'))
    mode_spec = P(('sys', 'ydom'), 'zdom', None)
    x_table, z_table = dft_tables()

    def local_energy(charge, real_mask, grid_idx, spline_w, influence):
        slots = charge.shape[0]
        blocks = slots // BLOCK
        vmem = pl.BlockSpec(memory_space=pltpu.VMEM)
        mode_energy, energy = pl.pallas_call(
            functools.partial(kernel, blocks),
            name='pme',
            out_shape=(jax.ShapeDtypeStruct(influence.shape, F32), jax.ShapeDtypeStruct((1,), F32)),
            in_specs=[vmem] * 7,
            out_specs=(vmem, pl.BlockSpec(memory_space=pltpu.SMEM)),
            scratch_shapes=[
                pltpu.VMEM((blocks, 2 * GRID, BLOCK), BF16),
                pltpu.VMEM((blocks, Y_ROWS, BLOCK), F32),
                pltpu.VMEM((blocks, LEN_Z, BLOCK), F32),
                pltpu.VMEM((8 * LEN_Z, GRID), F32),
                pltpu.VMEM((GHOST, LEN_Z, GRID), F32),
                pltpu.VMEM((GHOST, Y_ROWS, GRID), F32),
                pltpu.VMEM((GHOST, LEN_Z, GRID), F32),
                pltpu.VMEM((GHOST, LEN_Y, GRID), F32),
                pltpu.VMEM((GHOST, 8, GRID), F32),
                pltpu.VMEM((GROUPS, 2, 4, GRID, GRID), F32),
                pltpu.VMEM((4, GROUPS, CHUNKS, 2, 4, 8, GRID), F32),
                pltpu.VMEM((8, 8, 2, 8, GRID), F32),
                pltpu.VMEM((CHUNKS, 2, 64, 8, GRID), F32),
                pltpu.VMEM((CHUNKS, 64, 8, GRID), F32),
                pltpu.VMEM((8, GRID), F32),
                pltpu.VMEM((8, 8, GRID), F32),
                pltpu.SemaphoreType.DMA((3,)),
                pltpu.SemaphoreType.DMA((3,)),
                pltpu.SemaphoreType.DMA((GROUPS, CHUNKS, 4)),
                pltpu.SemaphoreType.DMA((GROUPS, CHUNKS, 4)),
                pltpu.SemaphoreType.DMA((CHUNKS,)),
                pltpu.SemaphoreType.DMA((CHUNKS,)),
                pltpu.SemaphoreType.DMA((8,)),
                pltpu.SemaphoreType.DMA((8,)),
            ],
            compiler_params=pltpu.CompilerParams(collective_id=0, has_side_effects=True, vmem_limit_bytes=56 * 1024 * 1024),
        )(charge.reshape(1, slots), real_mask.reshape(1, slots), grid_idx.T,
          jnp.transpose(spline_w, (1, 2, 0)), influence, jnp.asarray(x_table), jnp.asarray(z_table))
        return mode_energy, energy

    return jax.shard_map(local_energy, mesh=mesh, in_specs=(slot_spec, slot_spec, P(('sys', 'ydom', 'zdom'), None), P(('sys', 'ydom', 'zdom'), None, None), mode_spec), out_specs=(mode_spec, P('sys')), check_vma=False)
```

profile of v0, /device:TPU:0, one launch (start us, length us, event | category | flops | bytes accessed | tf_op | source)
XLA Modules:
  0.0 97.4 jit_solution(11528506372508411704)
XLA Ops:
  0.6 92.8 %pme.1 = (f32[32,64,128]{2,1,0:T(8,128)}, f32[1]{0:T(128)}) custom-call(f32[1,8192]{1,0:T(1,128)} %bitcast.6, s32[1,8192]{1,0:T(1,128)} %bitcast.7, s32[3,8192]{1,0:T(4,128)} %bitcast.5, f32[3,4,8192]{2,1,0:T(4,128)} %bitcast.4, f32[32,64,128]{2,1,0:T(8,128)} %influence.1, bf16[2,256,128]{2,1,0:T(8,128)(2,1)} %constant.4.clone.x_table, ...), custom_call_target="tpu_custom_call" | custom-call | tf_op jit(solution)/shard_map/pme/pallas_call | solution.py:278
  93.4 2.3 %copy.11 = f32[32,64,128]{2,1,0:T(8,128)} copy(f32[32,64,128]{2,1,0:T(8,128)} %get-tuple-element.4) | data formatting | bytes 2097152
where the time goes:
time: 97.6 us; the launch traced here: 97.4 us
  Pallas kernels  92.8 us (95%)
  between operations  2.33 us (2%)
  local copies, waits for them, and re-layouts  2.31 us (2%)
    pallas_call x1, Pallas kernels, local_energy(): pl.pallas_call(functools.partial(kernel, blocks), name='pme', out_shape=(...  92.8 us
    unnamed x1, local copies, waits for them, and re-layouts  2.31 us

commit v1 on v0

v1 whole, which is shorter than its diff:
```python
import functools
import math
import numpy as np
import jax
import jax.numpy as jnp
from jax import lax
from jax.experimental import pallas as pl
from jax.experimental.pallas import tpu as pltpu
from jax.sharding import PartitionSpec as P

MESH = pl.DeviceIdType.MESH
F32 = jnp.float32
BF16 = jnp.bfloat16
GRID = 128
LEN_Y = 32
LEN_Z = 64
GHOST = 3
BLOCK = 256
Y_ROWS = 40
CHUNKS = 4
UNROLL = 4
VMEM_LIMIT = 28 * 1024 * 1024
GROUP_B = ((2, 3), (4, 5), (0, 1), (6,), (7,))
PAIRS = tuple(tuple(bs) + tuple(8 + b for b in bs) for bs in GROUP_B)
OFFSET = tuple(sum(4 * len(p) + 1 for p in PAIRS[:g]) for g in range(len(PAIRS)))
TILES = sum(4 * len(p) + 1 for p in PAIRS)
PLACE = {pair: (g, OFFSET[g] + 4 * n) for g, pairs in enumerate(PAIRS) for n, pair in enumerate(pairs)}
NT = (((1,), (1,)), ((), ()))
NN = (((1,), (0,)), ((), ()))


def split_table(table):
    table = np.asarray(table, np.float32)
    high = table.astype(jnp.bfloat16)
    low = (table - high.astype(np.float32)).astype(jnp.bfloat16)
    return np.stack([high, low])


def dft_tables():
    k = np.arange(GRID)
    phase = 2.0 * np.pi * ((k[:, None] * k[None, :]) % GRID) / GRID
    cos, sin = np.cos(phase), np.sin(phase)
    x_table = np.concatenate([cos, -sin], axis=0)
    z_table = []
    for half in range(2):
        c = cos[64 * half:64 * half + 64]
        s = sin[64 * half:64 * half + 64]
        z_table.append(np.block([[c, -s], [s, c]]))
    return split_table(x_table), split_table(np.concatenate(z_table, axis=0))


def split(value):
    high = value.astype(BF16)
    low = (value - high.astype(F32)).astype(BF16)
    return high, low


def dot(a, b, dims):
    return lax.dot_general(a, b, dims, preferred_element_type=F32)


def taps(base, weights, rows):
    delta = lax.broadcasted_iota(jnp.int32, (rows, base.shape[1]), 0) - base
    out = jnp.where(delta == 3, weights[3:4], 0.0)
    for s in (2, 1, 0):
        out = jnp.where(delta == s, weights[s:s + 1], out)
    return out


def c_add(a, b):
    return a[0] + b[0], a[1] + b[1]


def c_sub(a, b):
    return a[0] - b[0], a[1] - b[1]


def c_mul(a, turn):
    turn = turn % 1.0
    if turn == 0.0:
        return a
    if turn == 0.25:
        return a[1], -a[0]
    if turn == 0.5:
        return -a[0], -a[1]
    if turn == 0.75:
        return -a[1], a[0]
    c, s = math.cos(2 * math.pi * turn), math.sin(2 * math.pi * turn)
    if turn == 0.125:
        return c * (a[0] + a[1]), c * (a[1] - a[0])
    return c * a[0] + s * a[1], c * a[1] - s * a[0]


def fft(values):
    n = len(values)
    if n == 1:
        return values
    even, odd = fft(values[0::2]), fft(values[1::2])
    turned = [c_mul(o, k / n) for k, o in enumerate(odd)]
    return [c_add(e, t) for e, t in zip(even, turned)] + [c_sub(e, t) for e, t in zip(even, turned)]


def kernel(blocks, charge, mask, index, spline, influence_hbm, x_table_hbm, z_table_hbm,
           energy_hbm, total_out,
           influence, x_table, z_table, energy,
           xcat, yline, zline, acc, yghost, zghost, yface, zface, corner,
           modes, fsend, grecv, scale, mid, hbuf, evec, erecv,
           load_sem, store_sem, ghost_send, ghost_recv, a_send, a_recv, e_send, e_recv):
    i = lax.axis_index('ydom')
    j = lax.axis_index('zdom')
    me = j * 4 + i
    i_next = lax.rem(i + 1, 4)
    j_next = 1 - j

    barrier = pltpu.get_barrier_semaphore()
    for off in range(1, 8):
        peer = lax.rem(me + off, 8)
        pl.semaphore_signal(barrier, inc=1, device_id=(0, peer // 4, lax.rem(peer, 4)), device_id_type=MESH)

    loads = [pltpu.make_async_copy(src, dst, load_sem.at[n]) for n, (src, dst) in enumerate(
        [(x_table_hbm, x_table), (z_table_hbm, z_table), (influence_hbm, influence)])]
    for copy in loads:
        copy.start()

    yghost[...] = jnp.zeros_like(yghost)
    zghost[...] = jnp.zeros_like(zghost)
    zface[GHOST * LEN_Y:] = jnp.zeros((5 * LEN_Y, GRID), F32)
    corner[GHOST * 8:] = jnp.zeros((5 * 8, GRID), F32)

    def prepare(step, carry):
        total = None
        for n in range(2):
            b = 2 * step + n
            lanes = pl.ds(pl.multiple_of(b * BLOCK, BLOCK), BLOCK)
            weight = charge[:, lanes] * mask[:, lanes].astype(F32)
            wx = spline[0, :, lanes] * weight
            delta = (lax.broadcasted_iota(jnp.int32, (GRID, BLOCK), 0) - index[0:1, lanes]) & (GRID - 1)
            line = jnp.where(delta == 3, wx[3:4], 0.0)
            for s in (2, 1, 0):
                line = jnp.where(delta == s, wx[s:s + 1], line)
            xhigh, xlow = split(line)
            xcat[b, 0:GRID] = xhigh
            xcat[b, GRID:2 * GRID] = xlow
            yl = taps(index[1:2, lanes], spline[1, :, lanes], Y_ROWS)
            yline[b] = yl
            zl = taps(index[2:3, lanes], spline[2, :, lanes], LEN_Z + 8)
            zline[b] = zl[0:LEN_Z]
            rows = [yl[LEN_Y + t:LEN_Y + t + 1] * zl[0:LEN_Z] for t in range(GHOST)]
            rows += [zl[LEN_Z + u:LEN_Z + u + 1] * yl for u in range(GHOST)]
            rows += [jnp.zeros((8, BLOCK), F32)]
            high, low = split(jnp.concatenate(rows, axis=0))
            both = dot(high, jnp.concatenate([xhigh, xlow], axis=0), NT)
            part = both[:, 0:GRID] + both[:, GRID:] + dot(low, xhigh, NT)
            total = part if total is None else total + part
        yghost[...] += total[0:GHOST * LEN_Z].reshape(GHOST, LEN_Z, GRID)
        zghost[...] += total[GHOST * LEN_Z:GHOST * LEN_Z + GHOST * Y_ROWS].reshape(GHOST, Y_ROWS, GRID)
        return carry

    lax.fori_loop(0, blocks // 2, prepare, 0)

    pl.semaphore_wait(barrier, 7)
    ghosts = []
    for n, (src, dst, peer) in enumerate(
            [(yghost, yface, (0, j, i_next))]
            + [(zghost.at[u, 0:LEN_Y], zface.at[LEN_Y * u:LEN_Y * u + LEN_Y], (0, j_next, i)) for u in range(GHOST)]
            + [(zghost.at[u, LEN_Y:Y_ROWS], corner.at[8 * u:8 * u + 8], (0, j_next, i_next)) for u in range(GHOST)]):
        copy = pltpu.make_async_remote_copy(
            src_ref=src, dst_ref=dst, send_sem=ghost_send.at[n], recv_sem=ghost_recv.at[n],
            device_id=peer, device_id_type=MESH)
        copy.start()
        ghosts.append(copy)

    def spread_rows(pairs):
        count = 2 * LEN_Z * len(pairs)
        acc[0:count] = jnp.zeros((count, GRID), F32)

        def body(step, carry):
            both, single = None, None
            for n in range(UNROLL):
                b = UNROLL * step + n
                zl = zline[b]
                high, low = split(jnp.concatenate(
                    [yline[b, 2 * pair + h:2 * pair + h + 1] * zl for pair in pairs for h in range(2)], axis=0))
                one, two = dot(high, xcat[b], NT), dot(low, xcat[b, 0:GRID], NT)
                both, single = (one, two) if both is None else (both + one, single + two)
            acc[0:count] += both[:, 0:GRID] + both[:, GRID:] + single
            return carry
        lax.fori_loop(0, blocks // UNROLL, body, 0)

    a_copies = []
    for group, pairs in enumerate(PAIRS):
        spread_rows(pairs)
        if group == 0:
            for copy in ghosts:
                copy.wait_recv()
            loads[0].wait()
        for n, pair in enumerate(pairs):
            for h in range(2):
                y, row = 2 * pair + h, 64 * (2 * n + h)
                if y < GHOST:
                    acc[row:row + LEN_Z] += yface[y]
                    acc[row:row + 8] += corner[pl.ds(y, 8, stride=8)]
                acc[row:row + 8] += zface[pl.ds(y, 8, stride=LEN_Y)]
        for n in range(len(pairs)):
            high, low = split(acc[128 * n:128 * n + 128])
            modes[n] = dot(x_table[0], high, NT) + dot(x_table[1], high, NT) + dot(x_table[0], low, NT)
        first, last = OFFSET[group], OFFSET[group] + 4 * len(pairs)
        for peer in range(4):
            at = [(n, c, 32 * peer + 8 * c) for n in range(len(pairs)) for c in range(CHUNKS)]
            top = jnp.full((8, GRID), 1e-30, F32)
            for n, c, row in at:
                top = jnp.maximum(top, jnp.maximum(jnp.abs(modes[n, row:row + 8]), jnp.abs(modes[n, GRID + row:GRID + row + 8])))
            code = jnp.ceil(jnp.log(top) * 1024.0)
            inverse = 32760.0 / jnp.exp(code * (1.0 / 1024.0))
            for n, c, row in at:
                re = jnp.round(modes[n, row:row + 8] * inverse).astype(jnp.int32)
                im = jnp.round(modes[n, GRID + row:GRID + row + 8] * inverse).astype(jnp.int32)
                fsend[peer, first + 4 * n + c] = (im << 16) | (re & 0xffff)
            fsend[peer, last] = code.astype(jnp.int32)
        copies = []
        for d, dj in ((2, 1), (2, 0), (1, 1), (3, 1), (1, 0), (3, 0), (0, 1)):
            peer, peer_j = lax.rem(i + d, 4), (j_next if dj else j)
            copy = pltpu.make_async_remote_copy(
                src_ref=fsend.at[peer, first:last + 1], dst_ref=grecv.at[me, first:last + 1],
                send_sem=a_send.at[group, 2 * d + dj], recv_sem=a_recv.at[group, 2 * d + dj],
                device_id=(0, peer_j, peer), device_id_type=MESH)
            copy.start()
            copies.append(copy)
        a_copies.append(copies)
        grecv[me, first:last + 1] = fsend[i, first:last + 1]

    for group, bs in enumerate(GROUP_B):
        for copy in a_copies[group]:
            copy.wait_recv()
        last = OFFSET[group] + 4 * len(PAIRS[group])
        for src in range(8):
            scale[src, group] = jnp.exp(grecv[src, last].astype(F32) * (1.0 / 1024.0)) * (1.0 / 32760.0)

        def first_stage(part, carry):
            half, chunk = part // CHUNKS, lax.rem(part, CHUNKS)
            for b in bs:
                values = []
                for a in range(8):
                    src = 4 * half + a // 2
                    word = grecv[src, PLACE[8 * (a % 2) + b][1] + chunk]
                    unit = scale[src, group]
                    values.append((((word << 16) >> 16).astype(F32) * unit, (word >> 16).astype(F32) * unit))
                for c, value in enumerate(fft(values)):
                    value = c_mul(value, b * c / 64)
                    mid[part, c, b, 0] = value[0]
                    mid[part, c, b, 1] = value[1]
            return carry
        lax.fori_loop(0, 2 * CHUNKS, first_stage, 0)

    low_half = lax.broadcasted_iota(jnp.int32, (8, GRID), 1) < 64
    sign = (1 - 2 * j).astype(F32)
    loads[1].wait()
    loads[2].wait()

    def modes_of(chunk, total):
        for half in range(2):
            for c in range(8):
                values = fft([(mid[CHUNKS * half + chunk, c, b, 0], mid[CHUNKS * half + chunk, c, b, 1]) for b in range(8)])
                for d, value in enumerate(values):
                    k = c + 8 * d
                    turned = c_mul(value, k / 128)
                    left = jnp.where(low_half, value[0], pltpu.roll(value[1], 64, 1))
                    right = jnp.where(low_half, pltpu.roll(turned[0], 64, 1), turned[1])
                    hbuf[half, k] = left + sign * right
        rows = jnp.concatenate([hbuf[0].reshape(512, GRID), hbuf[1].reshape(512, GRID)], axis=1)
        high, low = split(rows)
        out = dot(high, z_table[0], NN) + dot(high, z_table[1], NN) + dot(low, z_table[0], NN)
        re, im = out[:, 0:GRID], out[:, GRID:]
        power = jnp.transpose((re * re + im * im).reshape(64, 8, GRID), (1, 0, 2))
        kx = pl.ds(pl.multiple_of(8 * chunk, 8), 8)
        mode = 0.5 * influence[kx] * power
        energy[kx] = mode
        pltpu.make_async_copy(energy.at[kx], energy_hbm.at[kx], store_sem.at[chunk]).start()
        return total + jnp.sum(mode.reshape(64, 8, GRID), axis=0)

    total = lax.fori_loop(0, CHUNKS, modes_of, jnp.zeros((8, GRID), F32))

    evec[...] = total
    e_copies = []
    for off in range(1, 8):
        peer = lax.rem(me + off, 8)
        copy = pltpu.make_async_remote_copy(
            src_ref=evec, dst_ref=erecv.at[me], send_sem=e_send.at[off], recv_sem=e_recv.at[off],
            device_id=(0, peer // 4, lax.rem(peer, 4)), device_id_type=MESH)
        copy.start()
        e_copies.append(copy)
    erecv[me] = total
    for copy in e_copies:
        copy.wait_recv()
    grand = erecv[0]
    for n in range(1, 8):
        grand = grand + erecv[n]
    total_out[0] = jnp.sum(grand) * (1.0 / (GRID * GRID * GRID))

    for copy in ghosts + [copy for copies in a_copies for copy in copies] + e_copies:
        copy.wait_send()
    for chunk in range(CHUNKS):
        kx = pl.ds(8 * chunk, 8)
        pltpu.make_async_copy(energy.at[kx], energy_hbm.at[kx], store_sem.at[chunk]).wait()


def solution(mesh):
    slot_spec = P(('sys', 'ydom', 'zdom'))
    mode_spec = P(('sys', 'ydom'), 'zdom', None)
    x_table, z_table = dft_tables()

    def local_energy(charge, real_mask, grid_idx, spline_w, influence):
        slots = charge.shape[0]
        blocks = slots // BLOCK
        vmem = pl.BlockSpec(memory_space=pltpu.VMEM)
        hbm = pl.BlockSpec(memory_space=pl.ANY)
        groups = len(PAIRS)
        return pl.pallas_call(
            functools.partial(kernel, blocks),
            name='pme',
            out_shape=(jax.ShapeDtypeStruct(influence.shape, F32), jax.ShapeDtypeStruct((1,), F32)),
            in_specs=[vmem] * 4 + [hbm] * 3,
            out_specs=(hbm, pl.BlockSpec(memory_space=pltpu.SMEM)),
            scratch_shapes=[
                pltpu.VMEM(influence.shape, F32),
                pltpu.VMEM(x_table.shape, BF16),
                pltpu.VMEM(z_table.shape, BF16),
                pltpu.VMEM(influence.shape, F32),
                pltpu.VMEM((blocks, 2 * GRID, BLOCK), BF16),
                pltpu.VMEM((blocks, Y_ROWS, BLOCK), F32),
                pltpu.VMEM((blocks, LEN_Z, BLOCK), F32),
                pltpu.VMEM((max(map(len, PAIRS)) * 2 * LEN_Z, GRID), F32),
                pltpu.VMEM((GHOST, LEN_Z, GRID), F32),
                pltpu.VMEM((GHOST, Y_ROWS, GRID), F32),
                pltpu.VMEM((GHOST, LEN_Z, GRID), F32),
                pltpu.VMEM((8 * LEN_Y, GRID), F32),
                pltpu.VMEM((8 * 8, GRID), F32),
                pltpu.VMEM((max(map(len, PAIRS)), 2 * GRID, GRID), F32),
                pltpu.VMEM((4, TILES, 8, GRID), jnp.int32),
                pltpu.VMEM((8, TILES, 8, GRID), jnp.int32),
                pltpu.VMEM((8, groups, 8, GRID), F32),
                pltpu.VMEM((2 * CHUNKS, 8, 8, 2, 8, GRID), F32),
                pltpu.VMEM((2, 64, 8, GRID), F32),
                pltpu.VMEM((8, GRID), F32),
                pltpu.VMEM((8, 8, GRID), F32),
                pltpu.SemaphoreType.DMA((3,)),
                pltpu.SemaphoreType.DMA((CHUNKS,)),
                pltpu.SemaphoreType.DMA((7,)),
                pltpu.SemaphoreType.DMA((7,)),
                pltpu.SemaphoreType.DMA((groups, 8)),
                pltpu.SemaphoreType.DMA((groups, 8)),
                pltpu.SemaphoreType.DMA((8,)),
                pltpu.SemaphoreType.DMA((8,)),
            ],
            compiler_params=pltpu.CompilerParams(collective_id=0, has_side_effects=True, vmem_limit_bytes=VMEM_LIMIT),
        )(charge.reshape(1, slots), real_mask.reshape(1, slots), grid_idx.T,
          jnp.transpose(spline_w, (1, 2, 0)), influence, jnp.asarray(x_table), jnp.asarray(z_table))

    return jax.shard_map(local_energy, mesh=mesh, in_specs=(slot_spec, slot_spec, P(('sys', 'ydom', 'zdom'), None), P(('sys', 'ydom', 'zdom'), None, None), mode_spec), out_specs=(mode_spec, P('sys')), check_vma=False)
```

time: 97.6 us -> 61.6 us (0.63)
  Pallas kernels: 92.8 us -> 51.4 us
  local copies, waits for them, and re-layouts: 2.31 us -> 7.46 us
    pallas_call x1, Pallas kernels: 92.8 us -> 51.4 us  [local_energy(): pl.pallas_call(functools.partial(kernel, blocks), name='pme', out_shape=(...]
    unnamed x1 -> x15, local copies, waits for them, and re-layouts: 2.31 us -> 7.46 us
where the time goes in v1:
time: 61.6 us; the launch traced here: 61.2 us
  Pallas kernels  51.4 us (83%)
  local copies, waits for them, and re-layouts  7.46 us (12%)
  between operations  2.34 us (4%)
    pallas_call x1, Pallas kernels, local_energy(): pl.pallas_call(functools.partial(kernel, blocks), name='pme', out_shape=(...  51.4 us
    unnamed x15, local copies, waits for them, and re-layouts  7.46 us

profile of v1, /device:TPU:0, one launch (start us, length us, event | category | flops | bytes accessed | tf_op | source)
XLA Modules:
  0.0 61.2 jit_solution(12836156117179667257)
XLA Ops:
  0.6 0.0 copy-start
  0.6 1.2 %copy-done = f32[32,64,128]{2,1,0:T(8,128)S(1)} copy-done((f32[32,64,128]{2,1,0:T(8,128)S(1)}, f32[32,64,128]{2,1,0:T(8,128)}, u32[]{:S(2)}) %copy-start) | copy-done | bytes 1048600
  1.9 0.0 copy-start.1
  1.9 1.0 %copy-done.1 = f32[8192,3,4]{0,2,1:T(4,128)S(1)} copy-done((f32[8192,3,4]{0,2,1:T(4,128)S(1)}, f32[8192,3,4]{0,2,1:T(4,128)}, u32[]{:S(2)}) %copy-start.1) | copy-done | bytes 393240
  2.9 0.0 copy-start.2
  2.9 0.9 %copy-done.2 = bf16[2,256,256]{2,1,0:T(8,128)(2,1)S(1)} copy-done((bf16[2,256,256]{2,1,0:T(8,128)(2,1)S(1)}, bf16[2,256,256]{2,1,0:T(8,128)(2,1)}, u32[]{:S(2)}) %copy-start.2) | copy-done | bytes 262168
  3.8 0.0 copy-start.3
  3.8 0.9 %copy-done.3 = s32[8192,3]{0,1:T(4,128)S(1)} copy-done((s32[8192,3]{0,1:T(4,128)S(1)}, s32[8192,3]{0,1:T(4,128)}, u32[]{:S(2)}) %copy-start.3) | copy-done | bytes 98328
  4.7 0.0 copy-start.4
  4.7 0.9 %copy-done.4 = bf16[2,256,128]{2,1,0:T(8,128)(2,1)S(1)} copy-done((bf16[2,256,128]{2,1,0:T(8,128)(2,1)S(1)}, bf16[2,256,128]{2,1,0:T(8,128)(2,1)}, u32[]{:S(2)}) %copy-start.4) | copy-done | bytes 131096
  5.6 0.0 copy-start.5
  5.6 0.8 %copy-done.5 = f32[8192]{0:T(1024)S(1)} copy-done((f32[8192]{0:T(1024)S(1)}, f32[8192]{0:T(1024)}, u32[]{:S(2)}) %copy-start.5) | copy-done | bytes 32792
  6.4 0.0 copy-start.6
  6.4 0.8 %copy-done.6 = s32[8192]{0:T(1024)S(1)} copy-done((s32[8192]{0:T(1024)S(1)}, s32[8192]{0:T(1024)}, u32[]{:S(2)}) %copy-start.6) | copy-done | bytes 32792
  7.1 51.4 %pme.1 = (f32[32,64,128]{2,1,0:T(8,128)S(1)}, f32[1]{0:T(128)}) custom-call(f32[1,8192]{1,0:T(1,128)S(1)} %bitcast.6, s32[1,8192]{1,0:T(1,128)S(1)} %bitcast.7, s32[3,8192]{1,0:T(4,128)S(1)} %bitcast.5, f32[3,4,8192]{2,1,0:T(4,128)S(1)} %bitcast.4, f32[32,64,128]{2,1,0:T(8,128)S(1)} %copy-done, bf16[2,256,128]{2,1,0:T(8,128)(2,1)S(1)} %copy-done.4, ...), custom_call_target="tpu_custom_call" | custom-call | tf_op jit(solution)/shard_map/pme/pallas_call | solution.py:318
  58.5 1.0 %copy.11 = f32[32,64,128]{2,1,0:T(8,128)} copy(f32[32,64,128]{2,1,0:T(8,128)S(1)} %get-tuple-element.4) | data formatting | bytes 2097152
Async XLA Ops:
  0.6 1.2 %copy-start = (f32[32,64,128]{2,1,0:T(8,128)S(1)}, f32[32,64,128]{2,1,0:T(8,128)}, u32[]{:S(2)}) copy-start(f32[32,64,128]{2,1,0:T(8,128)} %influence_hbm.1) | copy-start | bytes 3145732
  1.9 1.0 %copy-start.1 = (f32[8192,3,4]{0,2,1:T(4,128)S(1)}, f32[8192,3,4]{0,2,1:T(4,128)}, u32[]{:S(2)}) copy-start(f32[8192,3,4]{0,2,1:T(4,128)} %param.10) | copy-start | bytes 1179652
  2.9 0.9 %copy-start.2 = (bf16[2,256,256]{2,1,0:T(8,128)(2,1)S(1)}, bf16[2,256,256]{2,1,0:T(8,128)(2,1)}, u32[]{:S(2)}) copy-start(bf16[2,256,256]{2,1,0:T(8,128)(2,1)} %constant.5.clone.z_table_hbm) | copy-start | bytes 786436
  3.8 0.9 %copy-start.3 = (s32[8192,3]{0,1:T(4,128)S(1)}, s32[8192,3]{0,1:T(4,128)}, u32[]{:S(2)}) copy-start(s32[8192,3]{0,1:T(4,128)} %param.9) | copy-start | bytes 294916
  4.7 0.9 %copy-start.4 = (bf16[2,256,128]{2,1,0:T(8,128)(2,1)S(1)}, bf16[2,256,128]{2,1,0:T(8,128)(2,1)}, u32[]{:S(2)}) copy-start(bf16[2,256,128]{2,1,0:T(8,128)(2,1)} %constant.4.clone.x_table_hbm) | copy-start | bytes 393220
  5.6 0.8 %copy-start.5 = (f32[8192]{0:T(1024)S(1)}, f32[8192]{0:T(1024)}, u32[]{:S(2)}) copy-start(f32[8192]{0:T(1024)} %param.7) | copy-start | bytes 98308
  6.4 0.8 %copy-start.6 = (s32[8192]{0:T(1024)S(1)}, s32[8192]{0:T(1024)}, u32[]{:S(2)}) copy-start(s32[8192]{0:T(1024)} %param.8) | copy-start | bytes 98308

commit v2 on v1

--- a/solution.py
+++ b/solution.py
@@ -19,8 +19,8 @@
 Y_ROWS = 40
 CHUNKS = 4
 UNROLL = 4
-VMEM_LIMIT = 28 * 1024 * 1024
-GROUP_B = ((2, 3), (4, 5), (0, 1), (6,), (7,))
+VMEM_LIMIT = 60 * 1024 * 1024
+GROUP_B = ((2,), (3, 4), (5, 6), (0, 1), (7,))
 PAIRS = tuple(tuple(bs) + tuple(8 + b for b in bs) for bs in GROUP_B)
 OFFSET = tuple(sum(4 * len(p) + 1 for p in PAIRS[:g]) for g in range(len(PAIRS)))
 TILES = sum(4 * len(p) + 1 for p in PAIRS)
@@ -100,9 +100,9 @@
     return [c_add(e, t) for e, t in zip(even, turned)] + [c_sub(e, t) for e, t in zip(even, turned)]
 
 
-def kernel(blocks, charge, mask, index, spline, influence_hbm, x_table_hbm, z_table_hbm,
+def kernel(blocks, charge_hbm, mask_hbm, index_hbm, spline_hbm, influence_hbm, x_table_hbm, z_table_hbm,
            energy_hbm, total_out,
-           influence, x_table, z_table, energy,
+           charge, mask, index, spline, influence, x_table, z_table, energy,
            xcat, yline, zline, acc, yghost, zghost, yface, zface, corner,
            modes, fsend, grecv, scale, mid, hbuf, evec, erecv,
            load_sem, store_sem, ghost_send, ghost_recv, a_send, a_recv, e_send, e_recv):
@@ -118,7 +118,8 @@
         pl.semaphore_signal(barrier, inc=1, device_id=(0, peer // 4, lax.rem(peer, 4)), device_id_type=MESH)
 
     loads = [pltpu.make_async_copy(src, dst, load_sem.at[n]) for n, (src, dst) in enumerate(
-        [(x_table_hbm, x_table), (z_table_hbm, z_table), (influence_hbm, influence)])]
+        [(spline_hbm, spline), (index_hbm, index), (charge_hbm, charge), (mask_hbm, mask),
+         (x_table_hbm, x_table), (z_table_hbm, z_table), (influence_hbm, influence)])]
     for copy in loads:
         copy.start()
 
@@ -126,6 +127,8 @@
     zghost[...] = jnp.zeros_like(zghost)
     zface[GHOST * LEN_Y:] = jnp.zeros((5 * LEN_Y, GRID), F32)
     corner[GHOST * 8:] = jnp.zeros((5 * 8, GRID), F32)
+    for copy in loads[:4]:
+        copy.wait()
 
     def prepare(step, carry):
         total = None
@@ -193,7 +196,7 @@
         if group == 0:
             for copy in ghosts:
                 copy.wait_recv()
-            loads[0].wait()
+            loads[4].wait()
         for n, pair in enumerate(pairs):
             for h in range(2):
                 y, row = 2 * pair + h, 64 * (2 * n + h)
@@ -254,8 +257,8 @@
 
     low_half = lax.broadcasted_iota(jnp.int32, (8, GRID), 1) < 64
     sign = (1 - 2 * j).astype(F32)
-    loads[1].wait()
-    loads[2].wait()
+    loads[5].wait()
+    loads[6].wait()
 
     def modes_of(chunk, total):
         for half in range(2):
@@ -312,16 +315,19 @@
     def local_energy(charge, real_mask, grid_idx, spline_w, influence):
         slots = charge.shape[0]
         blocks = slots // BLOCK
-        vmem = pl.BlockSpec(memory_space=pltpu.VMEM)
-        hbm = pl.BlockSpec(memory_space=pl.ANY)
+        hbm = pl.BlockSpec(memory_space=pltpu.HBM)
         groups = len(PAIRS)
         return pl.pallas_call(
             functools.partial(kernel, blocks),
             name='pme',
             out_shape=(jax.ShapeDtypeStruct(influence.shape, F32), jax.ShapeDtypeStruct((1,), F32)),
-            in_specs=[vmem] * 4 + [hbm] * 3,
-            out_specs=(hbm, pl.BlockSpec(memory_space=pltpu.SMEM)),
+            in_specs=[hbm] * 7,
+            out_specs=(pl.BlockSpec(memory_space=pl.ANY), pl.BlockSpec(memory_space=pltpu.SMEM)),
             scratch_shapes=[
+                pltpu.VMEM((1, slots), F32),
+                pltpu.VMEM((1, slots), jnp.int32),
+                pltpu.VMEM((3, slots), jnp.int32),
+                pltpu.VMEM((3, 4, slots), F32),
                 pltpu.VMEM(influence.shape, F32),
                 pltpu.VMEM(x_table.shape, BF16),
                 pltpu.VMEM(z_table.shape, BF16),
@@ -343,7 +349,7 @@
                 pltpu.VMEM((2, 64, 8, GRID), F32),
                 pltpu.VMEM((8, GRID), F32),
                 pltpu.VMEM((8, 8, GRID), F32),
-                pltpu.SemaphoreType.DMA((3,)),
+                pltpu.SemaphoreType.DMA((7,)),
                 pltpu.SemaphoreType.DMA((CHUNKS,)),
                 pltpu.SemaphoreType.DMA((7,)),
                 pltpu.SemaphoreType.DMA((7,)),

time: 61.6 us -> 57.9 us (0.940)
  local copies, waits for them, and re-layouts: 7.46 us -> 2.31 us
  Pallas kernels: 51.4 us -> 53.1 us
    unnamed x15 -> x1, local copies, waits for them, and re-layouts: 7.46 us -> 2.31 us
    pallas_call x1, Pallas kernels: 51.4 us -> 53.1 us  [local_energy(): pl.pallas_call(functools.partial(kernel, blocks), name='pme', out_shape=(...]
where the time goes in v2:
time: 57.9 us; the launch traced here: 57.7 us
  Pallas kernels  53.1 us (92%)
  between operations  2.33 us (4%)
  local copies, waits for them, and re-layouts  2.31 us (4%)
    pallas_call x1, Pallas kernels, local_energy(): pl.pallas_call(functools.partial(kernel, blocks), name='pme', out_shape=(...  53.1 us
    unnamed x1, local copies, waits for them, and re-layouts  2.31 us

profile of v2, /device:TPU:0, one launch (start us, length us, event | category | flops | bytes accessed | tf_op | source)
XLA Modules:
  0.0 57.7 jit_solution(15198044665212798731)
XLA Ops:
  0.6 53.1 %pme.1 = (f32[32,64,128]{2,1,0:T(8,128)}, f32[1]{0:T(128)}) custom-call(f32[1,8192]{1,0:T(1,128)} %bitcast.6, s32[1,8192]{1,0:T(1,128)} %bitcast.7, s32[3,8192]{1,0:T(4,128)} %bitcast.5, f32[3,4,8192]{2,1,0:T(4,128)} %bitcast.4, f32[32,64,128]{2,1,0:T(8,128)} %influence_hbm.1, bf16[2,256,128]{2,1,0:T(8,128)(2,1)} %constant.4.clone.x_table_hbm, ...), custom_call_target="tpu_custom_call" | custom-call | tf_op jit(solution)/shard_map/pme/pallas_call | solution.py:320
  53.7 2.3 %copy.11 = f32[32,64,128]{2,1,0:T(8,128)} copy(f32[32,64,128]{2,1,0:T(8,128)} %get-tuple-element.4) | data formatting | bytes 2097152

commit v3 on v2

--- a/solution.py
+++ b/solution.py
@@ -19,7 +19,7 @@
 Y_ROWS = 40
 CHUNKS = 4
 UNROLL = 4
-VMEM_LIMIT = 60 * 1024 * 1024
+VMEM_LIMIT = 28 * 1024 * 1024
 GROUP_B = ((2,), (3, 4), (5, 6), (0, 1), (7,))
 PAIRS = tuple(tuple(bs) + tuple(8 + b for b in bs) for bs in GROUP_B)
 OFFSET = tuple(sum(4 * len(p) + 1 for p in PAIRS[:g]) for g in range(len(PAIRS)))
@@ -101,16 +101,18 @@
 
 
 def kernel(blocks, charge_hbm, mask_hbm, index_hbm, spline_hbm, influence_hbm, x_table_hbm, z_table_hbm,
-           energy_hbm, total_out,
-           charge, mask, index, spline, influence, x_table, z_table, energy,
+           energy, total_out,
+           charge, mask, index, spline, influence, x_table, z_table,
            xcat, yline, zline, acc, yghost, zghost, yface, zface, corner,
            modes, fsend, grecv, scale, mid, hbuf, evec, erecv,
-           load_sem, store_sem, ghost_send, ghost_recv, a_send, a_recv, e_send, e_recv):
+           load_sem, ghost_send, ghost_recv, a_send, a_recv, e_send, e_recv):
     i = lax.axis_index('ydom')
     j = lax.axis_index('zdom')
     me = j * 4 + i
     i_next = lax.rem(i + 1, 4)
     j_next = 1 - j
+    mate = i + 1 - 2 * lax.rem(i, 2)
+    cross, cross_mate = lax.rem(i + 2, 4), lax.rem(mate + 2, 4)
 
     barrier = pltpu.get_barrier_semaphore()
     for off in range(1, 8):
@@ -221,11 +223,11 @@
                 fsend[peer, first + 4 * n + c] = (im << 16) | (re & 0xffff)
             fsend[peer, last] = code.astype(jnp.int32)
         copies = []
-        for d, dj in ((2, 1), (2, 0), (1, 1), (3, 1), (1, 0), (3, 0), (0, 1)):
-            peer, peer_j = lax.rem(i + d, 4), (j_next if dj else j)
+        for n, (peer, peer_j) in enumerate(((cross, j), (i, j_next), (cross_mate, j), (mate, j_next), (mate, j),
+                                            (cross, j_next), (cross_mate, j_next))):
             copy = pltpu.make_async_remote_copy(
                 src_ref=fsend.at[peer, first:last + 1], dst_ref=grecv.at[me, first:last + 1],
-                send_sem=a_send.at[group, 2 * d + dj], recv_sem=a_recv.at[group, 2 * d + dj],
+                send_sem=a_send.at[group, n], recv_sem=a_recv.at[group, n],
                 device_id=(0, peer_j, peer), device_id_type=MESH)
             copy.start()
             copies.append(copy)
@@ -278,7 +280,6 @@
         kx = pl.ds(pl.multiple_of(8 * chunk, 8), 8)
         mode = 0.5 * influence[kx] * power
         energy[kx] = mode
-        pltpu.make_async_copy(energy.at[kx], energy_hbm.at[kx], store_sem.at[chunk]).start()
         return total + jnp.sum(mode.reshape(64, 8, GRID), axis=0)
 
     total = lax.fori_loop(0, CHUNKS, modes_of, jnp.zeros((8, GRID), F32))
@@ -302,9 +303,6 @@
 
     for copy in ghosts + [copy for copies in a_copies for copy in copies] + e_copies:
         copy.wait_send()
-    for chunk in range(CHUNKS):
-        kx = pl.ds(8 * chunk, 8)
-        pltpu.make_async_copy(energy.at[kx], energy_hbm.at[kx], store_sem.at[chunk]).wait()
 
 
 def solution(mesh):
@@ -322,7 +320,7 @@
             name='pme',
             out_shape=(jax.ShapeDtypeStruct(influence.shape, F32), jax.ShapeDtypeStruct((1,), F32)),
             in_specs=[hbm] * 7,
-            out_specs=(pl.BlockSpec(memory_space=pl.ANY), pl.BlockSpec(memory_space=pltpu.SMEM)),
+            out_specs=(pl.BlockSpec(memory_space=pltpu.VMEM), pl.BlockSpec(memory_space=pltpu.SMEM)),
             scratch_shapes=[
                 pltpu.VMEM((1, slots), F32),
                 pltpu.VMEM((1, slots), jnp.int32),
@@ -331,7 +329,6 @@
                 pltpu.VMEM(influence.shape, F32),
                 pltpu.VMEM(x_table.shape, BF16),
                 pltpu.VMEM(z_table.shape, BF16),
-                pltpu.VMEM(influence.shape, F32),
                 pltpu.VMEM((blocks, 2 * GRID, BLOCK), BF16),
                 pltpu.VMEM((blocks, Y_ROWS, BLOCK), F32),
                 pltpu.VMEM((blocks, LEN_Z, BLOCK), F32),
@@ -350,7 +347,6 @@
                 pltpu.VMEM((8, GRID), F32),
                 pltpu.VMEM((8, 8, GRID), F32),
                 pltpu.SemaphoreType.DMA((7,)),
-                pltpu.SemaphoreType.DMA((CHUNKS,)),
                 pltpu.SemaphoreType.DMA((7,)),
                 pltpu.SemaphoreType.DMA((7,)),
                 pltpu.SemaphoreType.DMA((groups, 8)),
@@ -359,7 +355,8 @@
                 pltpu.SemaphoreType.DMA((8,)),
             ],
             compiler_params=pltpu.CompilerParams(collective_id=0, has_side_effects=True, vmem_limit_bytes=VMEM_LIMIT),
-        )(charge.reshape(1, slots), real_mask.reshape(1, slots), grid_idx.T,
-          jnp.transpose(spline_w, (1, 2, 0)), influence, jnp.asarray(x_table), jnp.asarray(z_table))
+        )(*[pltpu.with_memory_space_constraint(value, pltpu.HBM) for value in (
+            charge.reshape(1, slots), real_mask.reshape(1, slots), grid_idx.T,
+            jnp.transpose(spline_w, (1, 2, 0)), influence, jnp.asarray(x_table), jnp.asarray(z_table))])
 
     return jax.shard_map(local_energy, mesh=mesh, in_specs=(slot_spec, slot_spec, P(('sys', 'ydom', 'zdom'), None), P(('sys', 'ydom', 'zdom'), None, None), mode_spec), out_specs=(mode_spec, P('sys')), check_vma=False)

time: 57.9 us -> 56.3 us (0.972)
  local copies, waits for them, and re-layouts: 2.31 us -> 0.97 us
    unnamed x1, local copies, waits for them, and re-layouts: 2.31 us -> 0.97 us
where the time goes in v3:
time: 56.3 us; the launch traced here: 56.2 us
  Pallas kernels  52.9 us (94%)
  between operations  2.33 us (4%)
  local copies, waits for them, and re-layouts  0.97 us (2%)
    pallas_call x1, Pallas kernels, local_energy(): pl.pallas_call(functools.partial(kernel, blocks), name='pme', out_shape=(...  52.9 us

profile of v3, /device:TPU:0, one launch (start us, length us, event | category | flops | bytes accessed | tf_op | source)
XLA Modules:
  0.0 56.2 jit_solution(14944029249370448303)
XLA Ops:
  0.6 52.9 %pme.1 = (f32[32,64,128]{2,1,0:T(8,128)S(1)}, f32[1]{0:T(128)}) custom-call(f32[1,8192]{1,0:T(1,128)} %bitcast.6, s32[1,8192]{1,0:T(1,128)} %bitcast.7, s32[3,8192]{1,0:T(4,128)} %bitcast.5, f32[3,4,8192]{2,1,0:T(4,128)} %bitcast.4, f32[32,64,128]{2,1,0:T(8,128)} %influence_hbm.1, bf16[2,256,128]{2,1,0:T(8,128)(2,1)} %constant.4.clone.x_table_hbm, ...), custom_call_target="tpu_custom_call" | custom-call | tf_op jit(solution)/shard_map/pme/pallas_call | solution.py:318
  53.5 1.0 %copy.11 = f32[32,64,128]{2,1,0:T(8,128)} copy(f32[32,64,128]{2,1,0:T(8,128)S(1)} %get-tuple-element.4) | data formatting | bytes 2097152

commit v4 on v3

--- a/solution.py
+++ b/solution.py
@@ -18,13 +18,13 @@
 BLOCK = 256
 Y_ROWS = 40
 CHUNKS = 4
-UNROLL = 4
+UNROLL = 8
 VMEM_LIMIT = 28 * 1024 * 1024
-GROUP_B = ((2,), (3, 4), (5, 6), (0, 1), (7,))
+GROUP_B = ((2, 3), (4, 5), (0, 1), (6,), (7,))
 PAIRS = tuple(tuple(bs) + tuple(8 + b for b in bs) for bs in GROUP_B)
 OFFSET = tuple(sum(4 * len(p) + 1 for p in PAIRS[:g]) for g in range(len(PAIRS)))
 TILES = sum(4 * len(p) + 1 for p in PAIRS)
-PLACE = {pair: (g, OFFSET[g] + 4 * n) for g, pairs in enumerate(PAIRS) for n, pair in enumerate(pairs)}
+PLACE = {pair: (OFFSET[g] + 1 + n, len(pairs)) for g, pairs in enumerate(PAIRS) for n, pair in enumerate(pairs)}
 NT = (((1,), (1,)), ((), ()))
 NN = (((1,), (0,)), ((), ()))
 
@@ -209,7 +209,7 @@
         for n in range(len(pairs)):
             high, low = split(acc[128 * n:128 * n + 128])
             modes[n] = dot(x_table[0], high, NT) + dot(x_table[1], high, NT) + dot(x_table[0], low, NT)
-        first, last = OFFSET[group], OFFSET[group] + 4 * len(pairs)
+        first, count = OFFSET[group], len(pairs)
         for peer in range(4):
             at = [(n, c, 32 * peer + 8 * c) for n in range(len(pairs)) for c in range(CHUNKS)]
             top = jnp.full((8, GRID), 1e-30, F32)
@@ -220,42 +220,55 @@
             for n, c, row in at:
                 re = jnp.round(modes[n, row:row + 8] * inverse).astype(jnp.int32)
                 im = jnp.round(modes[n, GRID + row:GRID + row + 8] * inverse).astype(jnp.int32)
-                fsend[peer, first + 4 * n + c] = (im << 16) | (re & 0xffff)
-            fsend[peer, last] = code.astype(jnp.int32)
-        copies = []
-        for n, (peer, peer_j) in enumerate(((cross, j), (i, j_next), (cross_mate, j), (mate, j_next), (mate, j),
-                                            (cross, j_next), (cross_mate, j_next))):
-            copy = pltpu.make_async_remote_copy(
-                src_ref=fsend.at[peer, first:last + 1], dst_ref=grecv.at[me, first:last + 1],
-                send_sem=a_send.at[group, n], recv_sem=a_recv.at[group, n],
-                device_id=(0, peer_j, peer), device_id_type=MESH)
-            copy.start()
-            copies.append(copy)
-        a_copies.append(copies)
-        grecv[me, first:last + 1] = fsend[i, first:last + 1]
-
-    for group, bs in enumerate(GROUP_B):
+                fsend[peer, first + 1 + count * c + n] = (im << 16) | (re & 0xffff)
+            fsend[peer, first] = code.astype(jnp.int32)
+        if group < len(PAIRS) - 1:
+            slabs = [(first, first + 1 + 4 * count)]
+        else:
+            slabs = [(first + 1 + count * c - (c == 0), first + 1 + count * (c + 1)) for c in range(CHUNKS)]
+        for start, stop in slabs:
+            copies = []
+            for n, (peer, peer_j) in enumerate(((cross, j), (i, j_next), (cross_mate, j), (mate, j_next), (mate, j),
+                                                (cross, j_next), (cross_mate, j_next))):
+                copy = pltpu.make_async_remote_copy(
+                    src_ref=fsend.at[peer, start:stop], dst_ref=grecv.at[me, start:stop],
+                    send_sem=a_send.at[len(a_copies), n], recv_sem=a_recv.at[len(a_copies), n],
+                    device_id=(0, peer_j, peer), device_id_type=MESH)
+                copy.start()
+                copies.append(copy)
+            a_copies.append(copies)
+        stop = first + 1 + 4 * count
+        grecv[me, first:stop] = fsend[i, first:stop]
+
+    def unit_of(group):
+        for src in range(8):
+            scale[src, group] = jnp.exp(grecv[src, OFFSET[group]].astype(F32) * (1.0 / 1024.0)) * (1.0 / 32760.0)
+
+    def first_stage(group, half, chunk):
+        part = CHUNKS * half + chunk
+        for b in GROUP_B[group]:
+            values = []
+            for a in range(8):
+                src = 4 * half + a // 2
+                tile, count = PLACE[8 * (a % 2) + b]
+                word = grecv[src, tile + count * chunk]
+                unit = scale[src, group]
+                values.append((((word << 16) >> 16).astype(F32) * unit, (word >> 16).astype(F32) * unit))
+            for c, value in enumerate(fft(values)):
+                value = c_mul(value, b * c / 64)
+                mid[part, c, b, 0] = value[0]
+                mid[part, c, b, 1] = value[1]
+
+    last = len(GROUP_B) - 1
+    for group in range(last):
         for copy in a_copies[group]:
             copy.wait_recv()
-        last = OFFSET[group] + 4 * len(PAIRS[group])
-        for src in range(8):
-            scale[src, group] = jnp.exp(grecv[src, last].astype(F32) * (1.0 / 1024.0)) * (1.0 / 32760.0)
-
-        def first_stage(part, carry):
-            half, chunk = part // CHUNKS, lax.rem(part, CHUNKS)
-            for b in bs:
-                values = []
-                for a in range(8):
-                    src = 4 * half + a // 2
-                    word = grecv[src, PLACE[8 * (a % 2) + b][1] + chunk]
-                    unit = scale[src, group]
-                    values.append((((word << 16) >> 16).astype(F32) * unit, (word >> 16).astype(F32) * unit))
-                for c, value in enumerate(fft(values)):
-                    value = c_mul(value, b * c / 64)
-                    mid[part, c, b, 0] = value[0]
-                    mid[part, c, b, 1] = value[1]
+        unit_of(group)
+
+        def stage_part(part, carry):
+            first_stage(group, part // CHUNKS, lax.rem(part, CHUNKS))
             return carry
-        lax.fori_loop(0, 2 * CHUNKS, first_stage, 0)
+        lax.fori_loop(0, 2 * CHUNKS, stage_part, 0)
 
     low_half = lax.broadcasted_iota(jnp.int32, (8, GRID), 1) < 64
     sign = (1 - 2 * j).astype(F32)
@@ -277,12 +290,20 @@
         out = dot(high, z_table[0], NN) + dot(high, z_table[1], NN) + dot(low, z_table[0], NN)
         re, im = out[:, 0:GRID], out[:, GRID:]
         power = jnp.transpose((re * re + im * im).reshape(64, 8, GRID), (1, 0, 2))
-        kx = pl.ds(pl.multiple_of(8 * chunk, 8), 8)
+        kx = pl.ds(8 * chunk, 8)
         mode = 0.5 * influence[kx] * power
         energy[kx] = mode
         return total + jnp.sum(mode.reshape(64, 8, GRID), axis=0)
 
-    total = lax.fori_loop(0, CHUNKS, modes_of, jnp.zeros((8, GRID), F32))
+    total = jnp.zeros((8, GRID), F32)
+    for chunk in range(CHUNKS):
+        for copy in a_copies[last + chunk]:
+            copy.wait_recv()
+        if chunk == 0:
+            unit_of(last)
+        for half in range(2):
+            first_stage(last, half, chunk)
+        total = modes_of(chunk, total)
 
     evec[...] = total
     e_copies = []
@@ -349,8 +370,8 @@
                 pltpu.SemaphoreType.DMA((7,)),
                 pltpu.SemaphoreType.DMA((7,)),
                 pltpu.SemaphoreType.DMA((7,)),
-                pltpu.SemaphoreType.DMA((groups, 8)),
-                pltpu.SemaphoreType.DMA((groups, 8)),
+                pltpu.SemaphoreType.DMA((groups + CHUNKS - 1, 7)),
+                pltpu.SemaphoreType.DMA((groups + CHUNKS - 1, 7)),
                 pltpu.SemaphoreType.DMA((8,)),
                 pltpu.SemaphoreType.DMA((8,)),
             ],

time: 56.3 us -> 53.3 us (0.947)
  Pallas kernels: 52.9 us -> 49.8 us
    pallas_call x1, Pallas kernels: 52.9 us -> 49.8 us  [local_energy(): pl.pallas_call(functools.partial(kernel, blocks), name='pme', out_shape=(...]
where the time goes in v4:
time: 53.3 us; the launch traced here: 53.1 us
  Pallas kernels  49.8 us (93%)
  between operations  2.33 us (4%)
  local copies, waits for them, and re-layouts  0.97 us (2%)
    pallas_call x1, Pallas kernels, local_energy(): pl.pallas_call(functools.partial(kernel, blocks), name='pme', out_shape=(...  49.8 us

profile of v4, /device:TPU:0, one launch (start us, length us, event | category | flops | bytes accessed | tf_op | source)
XLA Modules:
  0.0 53.1 jit_solution(5799546879601739398)
XLA Ops:
  0.6 49.8 %pme.1 = (f32[32,64,128]{2,1,0:T(8,128)S(1)}, f32[1]{0:T(128)}) custom-call(f32[1,8192]{1,0:T(1,128)} %bitcast.6, s32[1,8192]{1,0:T(1,128)} %bitcast.7, s32[3,8192]{1,0:T(4,128)} %bitcast.5, f32[3,4,8192]{2,1,0:T(4,128)} %bitcast.4, f32[32,64,128]{2,1,0:T(8,128)} %influence_hbm.1, bf16[2,256,128]{2,1,0:T(8,128)(2,1)} %constant.4.clone.x_table_hbm, ...), custom_call_target="tpu_custom_call" | custom-call | tf_op jit(solution)/shard_map/pme/pallas_call | solution.py:339
  50.5 1.0 %copy.11 = f32[32,64,128]{2,1,0:T(8,128)} copy(f32[32,64,128]{2,1,0:T(8,128)S(1)} %get-tuple-element.4) | data formatting | bytes 2097152

commit v5 on v4

--- a/solution.py
+++ b/solution.py
@@ -134,8 +134,8 @@
 
     def prepare(step, carry):
         total = None
-        for n in range(2):
-            b = 2 * step + n
+        for n in range(4):
+            b = 4 * step + n
             lanes = pl.ds(pl.multiple_of(b * BLOCK, BLOCK), BLOCK)
             weight = charge[:, lanes] * mask[:, lanes].astype(F32)
             wx = spline[0, :, lanes] * weight
@@ -154,14 +154,15 @@
             rows += [zl[LEN_Z + u:LEN_Z + u + 1] * yl for u in range(GHOST)]
             rows += [jnp.zeros((8, BLOCK), F32)]
             high, low = split(jnp.concatenate(rows, axis=0))
-            both = dot(high, jnp.concatenate([xhigh, xlow], axis=0), NT)
-            part = both[:, 0:GRID] + both[:, GRID:] + dot(low, xhigh, NT)
+            cat = jnp.concatenate([xhigh, xlow], axis=0)
+            part = dot(high, cat, NT) + dot(low, cat, NT)
             total = part if total is None else total + part
+        total = total[:, 0:GRID] + total[:, GRID:]
         yghost[...] += total[0:GHOST * LEN_Z].reshape(GHOST, LEN_Z, GRID)
         zghost[...] += total[GHOST * LEN_Z:GHOST * LEN_Z + GHOST * Y_ROWS].reshape(GHOST, Y_ROWS, GRID)
         return carry
 
-    lax.fori_loop(0, blocks // 2, prepare, 0)
+    lax.fori_loop(0, blocks // 4, prepare, 0)
 
     pl.semaphore_wait(barrier, 7)
     ghosts = []
@@ -180,15 +181,15 @@
         acc[0:count] = jnp.zeros((count, GRID), F32)
 
         def body(step, carry):
-            both, single = None, None
+            both = None
             for n in range(UNROLL):
                 b = UNROLL * step + n
                 zl = zline[b]
                 high, low = split(jnp.concatenate(
                     [yline[b, 2 * pair + h:2 * pair + h + 1] * zl for pair in pairs for h in range(2)], axis=0))
-                one, two = dot(high, xcat[b], NT), dot(low, xcat[b, 0:GRID], NT)
-                both, single = (one, two) if both is None else (both + one, single + two)
-            acc[0:count] += both[:, 0:GRID] + both[:, GRID:] + single
+                part = dot(high, xcat[b], NT) + dot(low, xcat[b], NT)
+                both = part if both is None else both + part
+            acc[0:count] += both[:, 0:GRID] + both[:, GRID:]
             return carry
         lax.fori_loop(0, blocks // UNROLL, body, 0)
 

time: 53.3 us -> 52.8 us (level)
  no operation moved by 1% of the time
where the time goes in v5:
time: 52.8 us; the launch traced here: 52.7 us
  Pallas kernels  49.4 us (94%)
  between operations  2.33 us (4%)
  local copies, waits for them, and re-layouts  0.97 us (2%)
    pallas_call x1, Pallas kernels, local_energy(): pl.pallas_call(functools.partial(kernel, blocks), name='pme', out_shape=(...  49.4 us

profile of v5, /device:TPU:0, one launch (start us, length us, event | category | flops | bytes accessed | tf_op | source)
XLA Modules:
  0.0 52.7 jit_solution(13663490355976854876)
XLA Ops:
  0.6 49.4 %pme.1 = (f32[32,64,128]{2,1,0:T(8,128)S(1)}, f32[1]{0:T(128)}) custom-call(f32[1,8192]{1,0:T(1,128)} %bitcast.6, s32[1,8192]{1,0:T(1,128)} %bitcast.7, s32[3,8192]{1,0:T(4,128)} %bitcast.5, f32[3,4,8192]{2,1,0:T(4,128)} %bitcast.4, f32[32,64,128]{2,1,0:T(8,128)} %influence_hbm.1, bf16[2,256,128]{2,1,0:T(8,128)(2,1)} %constant.4.clone.x_table_hbm, ...), custom_call_target="tpu_custom_call" | custom-call | tf_op jit(solution)/shard_map/pme/pallas_call | solution.py:340
  50.0 1.0 %copy.11 = f32[32,64,128]{2,1,0:T(8,128)} copy(f32[32,64,128]{2,1,0:T(8,128)S(1)} %get-tuple-element.4) | data formatting | bytes 2097152

commit v6 on v5

--- a/solution.py
+++ b/solution.py
@@ -143,9 +143,8 @@
             line = jnp.where(delta == 3, wx[3:4], 0.0)
             for s in (2, 1, 0):
                 line = jnp.where(delta == s, wx[s:s + 1], line)
-            xhigh, xlow = split(line)
-            xcat[b, 0:GRID] = xhigh
-            xcat[b, GRID:2 * GRID] = xlow
+            cat = jnp.concatenate(split(line.T), axis=1)
+            xcat[b] = cat
             yl = taps(index[1:2, lanes], spline[1, :, lanes], Y_ROWS)
             yline[b] = yl
             zl = taps(index[2:3, lanes], spline[2, :, lanes], LEN_Z + 8)
@@ -154,8 +153,7 @@
             rows += [zl[LEN_Z + u:LEN_Z + u + 1] * yl for u in range(GHOST)]
             rows += [jnp.zeros((8, BLOCK), F32)]
             high, low = split(jnp.concatenate(rows, axis=0))
-            cat = jnp.concatenate([xhigh, xlow], axis=0)
-            part = dot(high, cat, NT) + dot(low, cat, NT)
+            part = dot(high, cat, NN) + dot(low, cat, NN)
             total = part if total is None else total + part
         total = total[:, 0:GRID] + total[:, GRID:]
         yghost[...] += total[0:GHOST * LEN_Z].reshape(GHOST, LEN_Z, GRID)
@@ -187,7 +185,7 @@
                 zl = zline[b]
                 high, low = split(jnp.concatenate(
                     [yline[b, 2 * pair + h:2 * pair + h + 1] * zl for pair in pairs for h in range(2)], axis=0))
-                part = dot(high, xcat[b], NT) + dot(low, xcat[b], NT)
+                part = dot(high, xcat[b], NN) + dot(low, xcat[b], NN)
                 both = part if both is None else both + part
             acc[0:count] += both[:, 0:GRID] + both[:, GRID:]
             return carry
@@ -226,7 +224,7 @@
         if group < len(PAIRS) - 1:
             slabs = [(first, first + 1 + 4 * count)]
         else:
-            slabs = [(first + 1 + count * c - (c == 0), first + 1 + count * (c + 1)) for c in range(CHUNKS)]
+            slabs = [(first, first + 1 + 2 * count), (first + 1 + 2 * count, first + 1 + 4 * count)]
         for start, stop in slabs:
             copies = []
             for n, (peer, peer_j) in enumerate(((cross, j), (i, j_next), (cross_mate, j), (mate, j_next), (mate, j),
@@ -298,8 +296,9 @@
 
     total = jnp.zeros((8, GRID), F32)
     for chunk in range(CHUNKS):
-        for copy in a_copies[last + chunk]:
-            copy.wait_recv()
+        if chunk % 2 == 0:
+            for copy in a_copies[last + chunk // 2]:
+                copy.wait_recv()
         if chunk == 0:
             unit_of(last)
         for half in range(2):
@@ -351,7 +350,7 @@
                 pltpu.VMEM(influence.shape, F32),
                 pltpu.VMEM(x_table.shape, BF16),
                 pltpu.VMEM(z_table.shape, BF16),
-                pltpu.VMEM((blocks, 2 * GRID, BLOCK), BF16),
+                pltpu.VMEM((blocks, BLOCK, 2 * GRID), BF16),
                 pltpu.VMEM((blocks, Y_ROWS, BLOCK), F32),
                 pltpu.VMEM((blocks, LEN_Z, BLOCK), F32),
                 pltpu.VMEM((max(map(len, PAIRS)) * 2 * LEN_Z, GRID), F32),
@@ -371,8 +370,8 @@
                 pltpu.SemaphoreType.DMA((7,)),
                 pltpu.SemaphoreType.DMA((7,)),
                 pltpu.SemaphoreType.DMA((7,)),
-                pltpu.SemaphoreType.DMA((groups + CHUNKS - 1, 7)),
-                pltpu.SemaphoreType.DMA((groups + CHUNKS - 1, 7)),
+                pltpu.SemaphoreType.DMA((groups + 1, 7)),
+                pltpu.SemaphoreType.DMA((groups + 1, 7)),
                 pltpu.SemaphoreType.DMA((8,)),
                 pltpu.SemaphoreType.DMA((8,)),
             ],

time: 52.8 us -> 51.8 us (0.981)
  Pallas kernels: 49.4 us -> 48.4 us
    pallas_call x1, Pallas kernels: 49.4 us -> 48.4 us  [local_energy(): pl.pallas_call(functools.partial(kernel, blocks), name='pme', out_shape=(...]
where the time goes in v6:
time: 51.8 us; the launch traced here: 51.7 us
  Pallas kernels  48.4 us (93%)
  between operations  2.33 us (4%)
  local copies, waits for them, and re-layouts  0.97 us (2%)
    pallas_call x1, Pallas kernels, local_energy(): pl.pallas_call(functools.partial(kernel, blocks), name='pme', out_shape=(...  48.4 us

profile of v6, /device:TPU:0, one launch (start us, length us, event | category | flops | bytes accessed | tf_op | source)
XLA Modules:
  0.0 51.7 jit_solution(4618694631964472044)
XLA Ops:
  0.6 48.4 %pme.1 = (f32[32,64,128]{2,1,0:T(8,128)S(1)}, f32[1]{0:T(128)}) custom-call(f32[1,8192]{1,0:T(1,128)} %bitcast.6, s32[1,8192]{1,0:T(1,128)} %bitcast.7, s32[3,8192]{1,0:T(4,128)} %bitcast.5, f32[3,4,8192]{2,1,0:T(4,128)} %bitcast.4, f32[32,64,128]{2,1,0:T(8,128)} %influence_hbm.1, bf16[2,256,128]{2,1,0:T(8,128)(2,1)} %constant.4.clone.x_table_hbm, ...), custom_call_target="tpu_custom_call" | custom-call | tf_op jit(solution)/shard_map/pme/pallas_call | solution.py:339
  49.0 1.0 %copy.11 = f32[32,64,128]{2,1,0:T(8,128)} copy(f32[32,64,128]{2,1,0:T(8,128)S(1)} %get-tuple-element.4) | data formatting | bytes 2097152

commit v7 on v6

--- a/solution.py
+++ b/solution.py
@@ -18,7 +18,7 @@
 BLOCK = 256
 Y_ROWS = 40
 CHUNKS = 4
-UNROLL = 8
+UNROLL = 16
 VMEM_LIMIT = 28 * 1024 * 1024
 GROUP_B = ((2, 3), (4, 5), (0, 1), (6,), (7,))
 PAIRS = tuple(tuple(bs) + tuple(8 + b for b in bs) for bs in GROUP_B)

time: 51.8 us -> 51.4 us (level)
  no operation moved by 1% of the time
where the time goes in v7:
time: 51.4 us; the launch traced here: 51.3 us
  Pallas kernels  48 us (93%)
  between operations  2.33 us (5%)
  local copies, waits for them, and re-layouts  0.97 us (2%)
    pallas_call x1, Pallas kernels, local_energy(): pl.pallas_call(functools.partial(kernel, blocks), name='pme', out_shape=(...  48 us

profile of v7, /device:TPU:0, one launch (start us, length us, event | category | flops | bytes accessed | tf_op | source)
XLA Modules:
  0.0 51.3 jit_solution(10787701784716986525)
XLA Ops:
  0.6 48.0 %pme.1 = (f32[32,64,128]{2,1,0:T(8,128)S(1)}, f32[1]{0:T(128)}) custom-call(f32[1,8192]{1,0:T(1,128)} %bitcast.6, s32[1,8192]{1,0:T(1,128)} %bitcast.7, s32[3,8192]{1,0:T(4,128)} %bitcast.5, f32[3,4,8192]{2,1,0:T(4,128)} %bitcast.4, f32[32,64,128]{2,1,0:T(8,128)} %influence_hbm.1, bf16[2,256,128]{2,1,0:T(8,128)(2,1)} %constant.4.clone.x_table_hbm, ...), custom_call_target="tpu_custom_call" | custom-call | tf_op jit(solution)/shard_map/pme/pallas_call | solution.py:339
  48.6 1.0 %copy.11 = f32[32,64,128]{2,1,0:T(8,128)} copy(f32[32,64,128]{2,1,0:T(8,128)S(1)} %get-tuple-element.4) | data formatting | bytes 2097152
